TPU v7x, 32 devices: a whole 2x2x4 slice. The times are simulated.
32 devices in a mesh: space: 32 (over z, y, x, core), ens: 1.
Axes of the slice: x: 2, y: 2, z: 4, core: 2. Of those that a mesh axis runs over, the one named last changes fastest.
Arguments:
- innovations: bfloat16 [1, 2048, 128, 128], P('ens', 'space'), may hold values from -6 to 6
- block_owner: int32 [2048, 1], P('space'), may hold values from 0 to 31; in each aligned block of 64 rows (0 to 63, 64 to 127, ...) at most 4 rows name the same one
- block_tile: int32 [2048], P('space'), may hold values from 0 to 3
- block_count: int32 [32], P('space'), may hold values from 48 to 64
- obs_row: int32 [2048, 128], P('space'), may hold values from 0 to 6
- obs_col: int32 [2048, 128], P('space'), may hold values from 0 to 14
- offsets: float32 [2048, 2, 128], P('space'), may hold values from 0 to 1
- obs_mask: int32 [2048, 128], P('space'), may hold values 0 or 1
- sigma: float32 [128, 128], P('space'), may hold values from 0.3 to 3
- coupling: float32 [128, 128], replicated, may hold values from -0.5 to 0.5
Outputs:
- gradient: float32 [128, 128, 128], P('ens', 'space')
Inputs may be any that keep to these rules, and one draw needn't show every extreme that they name: `block_owner`: among the rows of one device, no owner is named more than 4 times, and one owner is named exactly 4 times in some devices' rows. `block_count`: blocks of a device at positions at or above its count are padding.
All inputs are finite; a program needn't handle non-finite values. No bound on the sum of `obs_mask` on one device may be relied on, other than what follows from the above.
Results may differ from a plain program's by a relative error of at most 0.0095.
Values may be sent and summed in bfloat16 or wider, within the bound.
A program may use at most 64 MiB of HBM per device.

v0:
```python
import jax
import jax.numpy as jnp
from jax import lax
from jax.sharding import PartitionSpec as P

TW = 16


def scaled_rows(totals, coupling, sigma, start, count, members):
    coupling_rows = lax.dynamic_slice_in_dim(coupling, start, count, 0)
    own = lax.dynamic_slice_in_dim(totals, start, count, 1)
    coupled = jnp.einsum("ck,tkh->cth", coupling_rows, totals, precision=lax.Precision.HIGHEST)
    return sigma[None, :, :] * (jnp.transpose(own, (1, 0, 2)) + coupled) / members


def accumulate_all(got_values, got_weights, got_places, tile_local, cell_count):
    group = 64
    width = got_values.shape[2]
    slot_total = got_values.shape[0]
    cell_ids = jnp.arange(cell_count, dtype=jnp.int32)
    tile_ids = jnp.arange(tile_local, dtype=jnp.int32)
    nothing = jnp.zeros((), got_values.dtype)
    exact = got_values.dtype == jnp.float32

    def accumulate(turn, totals):
        start = turn * group
        values = lax.dynamic_slice_in_dim(got_values, start, group, 0)
        weights = lax.dynamic_slice_in_dim(got_weights, start, group, 0)
        places = lax.dynamic_slice_in_dim(got_places, start, group, 0).astype(jnp.int32)
        base = places[:, 0, :] * TW + places[:, 1, :]
        offset = cell_ids[None, :, None] - base[:, None, :]
        table = jnp.where(
            offset == 0,
            weights[:, 0, :][:, None, :],
            jnp.where(
                offset == 1,
                weights[:, 1, :][:, None, :],
                jnp.where(
                    offset == TW,
                    weights[:, 2, :][:, None, :],
                    jnp.where(offset == TW + 1, weights[:, 3, :][:, None, :], nothing),
                ),
            ),
        )
        contrib = jnp.einsum("gco,goh->gch", table, values, preferred_element_type=jnp.float32)
        pick = (tile_ids[:, None] == places[None, :, 2, 0]).astype(jnp.float32)
        return totals + jnp.einsum("tg,gch->tch", pick, contrib, precision=lax.Precision.HIGHEST)

    return lax.fori_loop(
        0, slot_total // group, accumulate, jnp.zeros((tile_local, cell_count, width), jnp.float32)
    )


def on_device(
    innovations,
    block_owner,
    block_tile,
    block_count,
    obs_row,
    obs_col,
    offsets,
    obs_mask,
    sigma,
    coupling,
):
    peers = lax.axis_size("space")
    blk_local = innovations.shape[1]
    obs_count = innovations.shape[2]
    width = innovations.shape[3]
    tile_local = sigma.shape[0]
    cell_count = coupling.shape[0]
    capacity = max(2, 2 * blk_local // peers)
    slot_total = peers * capacity
    position = jnp.arange(blk_local, dtype=jnp.int32)
    alive = (position < block_count[0]).astype(jnp.float32)
    live = obs_mask.astype(jnp.float32) * alive[:, None]
    row_frac = offsets[:, 0, :]
    col_frac = offsets[:, 1, :]
    corner_weights = jnp.stack(
        [
            (1.0 - row_frac) * (1.0 - col_frac),
            (1.0 - row_frac) * col_frac,
            row_frac * (1.0 - col_frac),
            row_frac * col_frac,
        ],
        axis=1,
    )
    corner_weights = (corner_weights * live[:, None, :]).astype(jnp.bfloat16)
    tile_rows = jnp.broadcast_to(block_tile[:, None], obs_row.shape)
    placing = jnp.stack([obs_row, obs_col, tile_rows], axis=1)
    owner = block_owner[:, 0]
    earlier = (owner[:, None] == owner[None, :]) & (position[None, :] < position[:, None])
    slot = owner * capacity + jnp.sum(earlier.astype(jnp.int32), axis=1)
    ens_count = lax.axis_size("ens")
    members = ens_count * innovations.shape[0]
    share = cell_count // ens_count
    send_values = (
        jnp.zeros((slot_total, obs_count, width), jnp.bfloat16).at[slot].set(innovations[0])
    )
    send_weights = jnp.zeros((slot_total, 4, obs_count), jnp.bfloat16).at[slot].set(corner_weights)
    send_places = (
        jnp.zeros((slot_total, 3, obs_count), jnp.bfloat16)
        .at[slot]
        .set(placing.astype(jnp.bfloat16))
    )
    got_values, got_weights, got_places = (
        lax.all_to_all(send_values, "space", split_axis=0, concat_axis=0, tiled=True),
        lax.all_to_all(send_weights, "space", split_axis=0, concat_axis=0, tiled=True),
        lax.all_to_all(send_places, "space", split_axis=0, concat_axis=0, tiled=True),
    )
    totals = accumulate_all(got_values, got_weights, got_places, tile_local, cell_count)
    summed = lax.psum(totals.astype(jnp.bfloat16), "ens").astype(jnp.float32)
    first = lax.axis_index("ens") * share
    return scaled_rows(summed, coupling, sigma, first, share, members)


def solution(mesh):
    in_specs = (
        P("ens", "space", None, None),
        P("space", None),
        P("space"),
        P("space"),
        P("space", None),
        P("space", None),
        P("space", None, None),
        P("space", None),
        P("space", None),
        P(),
    )
    out_specs = P("ens", "space", None)
    return jax.shard_map(
        on_device, mesh=mesh, in_specs=in_specs, out_specs=out_specs, check_vma=False
    )
```

profile of v0, /device:TPU:0, one launch (start us, length us, event | category | flops | bytes accessed | tf_op | source)
XLA Modules:
  0.0 164.0 jit_solution(15709219192054505717)
XLA Ops:
  0.0 0.8 convert.15
  0.8 0.9 convert_reduce_fusion
  1.7 0.7 fusion.45
  2.4 0.8 convert_bitcast_fusion
  3.2 0.1 stack_broadcast_in_dim.2
  3.3 0.7 broadcast_in_dim.113
  4.0 7.7 %scatter_fusion = bf16[128,3,128]{2,1,0:T(4,128)(2,1)} fusion(bf16[128,3,128]{2,1,0:T(4,128)(2,1)} %broadcast_in_dim.113, s32[64]{0:T(128)S(1)} %fusion.45, bf16[64,3,128]{2,1,0:T(4,128)(2,1)S(1)} %copy.32), kind=kCustom, calls=%fused_computation | custom fusion | bytes 147712 | tf_op jit(solution)/shard_map/scatter | solution.py:104
  11.7 7.3 %all-to-all-start = ((bf16[128,3,128]{2,1,0:T(4,128)(2,1)}), bf16[128,3,128]{2,1,0:T(4,128)(2,1)S(1)}, u32[]{:S(2)}, u32[]{:S(2)}) async-start(bf16[128,3,128]{2,1,0:T(4,128)(2,1)} %scatter_fusion), calls=%async_computation | async-start | bytes 262144 | tf_op jit(solution)/shard_map/all_to_all | solution.py:109
  19.7 1.0 subtract_multiply_fusion.1
  20.8 0.8 convert_multiply_fusion
  21.6 0.1 fusion.41
  21.7 0.7 broadcast_in_dim.114
  22.4 7.4 %scatter_fusion.1 = bf16[128,4,128]{2,1,0:T(4,128)(2,1)} fusion(bf16[128,4,128]{2,1,0:T(4,128)(2,1)} %broadcast_in_dim.114, s32[64]{0:T(128)S(1)} %fusion.45, bf16[64,4,128]{2,1,0:T(4,128)(2,1)S(1)} %fusion.41), kind=kCustom, calls=%fused_computation.1 | custom fusion | bytes 196864 | tf_op jit(solution)/shard_map/scatter | solution.py:100
  29.8 5.9 %all-to-all-start.1 = ((bf16[128,4,128]{2,1,0:T(4,128)(2,1)}), bf16[128,4,128]{2,1,0:T(4,128)(2,1)S(1)}, u32[]{:S(2)}, u32[]{:S(2)}) async-start(bf16[128,4,128]{2,1,0:T(4,128)(2,1)} %scatter_fusion.1), calls=%async_computation.1 | async-start | bytes 262144 | tf_op jit(solution)/shard_map/all_to_all | solution.py:108
  35.7 3.0 %broadcast_in_dim.115 = bf16[128,128,128]{2,1,0:T(8,128)(2,1)} broadcast(bf16[]{:T(256)} %constant.64.clone.1), dimensions={} | broadcast | bytes 4194306 | tf_op jit(solution)/shard_map/broadcast_in_dim | solution.py:98
  38.7 8.7 %scatter_fusion.2 = bf16[128,128,128]{2,1,0:T(8,128)(2,1)} fusion(bf16[128,128,128]{2,1,0:T(8,128)(2,1)} %broadcast_in_dim.115, s32[64]{0:T(128)S(1)} %fusion.45, bf16[64,128,128]{2,1,0:T(8,128)(2,1)S(1)} %bitcast.54), kind=kCustom, calls=%fused_computation.2 | custom fusion | bytes 6291712 | tf_op jit(solution)/shard_map/scatter | solution.py:98
  47.4 6.0 %all-to-all-start.2 = ((bf16[128,128,128]{2,1,0:T(8,128)(2,1)}), bf16[128,128,128]{2,1,0:T(8,128)(2,1)}, u32[]{:S(2)}, u32[]{:S(2)}) async-start(bf16[128,128,128]{2,1,0:T(8,128)(2,1)} %scatter_fusion.2), calls=%async_computation.2 | async-start | bytes 8388608 | tf_op jit(solution)/shard_map/all_to_all | solution.py:107
  53.4 93.7 %all-to-all-done.2 = bf16[128,128,128]{2,1,0:T(8,128)(2,1)} async-done(((bf16[128,128,128]{2,1,0:T(8,128)(2,1)}), bf16[128,128,128]{2,1,0:T(8,128)(2,1)}, u32[]{:S(2)}, u32[]{:S(2)}) %all-to-all-start.2) | async-done | bytes 4194336 | tf_op jit(solution)/shard_map/all_to_all | solution.py:107
  147.1 15.6 %while.14 = (s32[]{:T(128)}, f32[4,128,128]{2,0,1:T(4,128)S(1)}, bf16[128,3,128]{2,1,0:T(4,128)(2,1)S(1)}, bf16[128,4,128]{2,1,0:T(4,128)(2,1)S(1)}, bf16[128,12...) while((s32[]{:T(128)}, f32[4,128,128]{2,0,1:T(4,128)S(1)}, ...), condition=%wide.region_5.6_spmd.clone, body=%wide.region_4.5_spmd.clone.sunk | while | flops 328376576 | bytes 11879409 | solution.py:49
  147.2 0.1 copy.59
  147.4 0.1 copy.60
  147.4 0.1 constant_dynamic-slice_fusion.8
  147.6 3.0 %fusion.59 = f32[64,128,128]{2,1,0:T(8,128)S(1)} fusion(bf16[128,128,128]{2,1,0:T(8,128)(2,1)} %get-tuple-element.266, s32[]{:T(128)S(6)} %select_n.85, s32[64,128]{1,0:T(8,128)S(1)} %copy.60, bf16[64,128]{1,0:T(8,128)(2,1)S(1)} %get-tuple-element.232, bf16[64,128]{1,0:T(8,128)(2,1)S(1)} %get-tuple-element.233, ...), kind=kOutput, calls=%fused_computation.16.clone.1 | convolution fusion | flops 277872640 | bytes 6389764 | tf_op jit(solution)/shard_map/while/body/eval_jaxpr/gco,goh->gch/dot_general | solution.py:45
  150.6 4.3 %fusion.60 = f32[4,128,128]{2,0,1:T(4,128)S(1)} fusion(f32[64,128,128]{2,1,0:T(8,128)S(1)} %fusion.59, f32[4,128,128]{2,0,1:T(4,128)S(1)} %get-tuple-element.251, pred[]{:T(512)S(6)} %compare.3, s32[64]{0:T(128)S(1)} %slice_bitcast_fusion.2), kind=kOutput, calls=%fused_computation.23.clone.1 | convolution fusion | flops 50462976 | bytes 4718849 | tf_op jit(solution)/shard_map/while/body/eval_jaxpr/tg,gch->tch/dot_general | solution.py:47
  154.9 0.1 copy.59
  155.1 0.1 copy.60
  155.2 0.1 constant_dynamic-slice_fusion.8
  155.4 3.0 %fusion.59 = f32[64,128,128]{2,1,0:T(8,128)S(1)} fusion(bf16[128,128,128]{2,1,0:T(8,128)(2,1)} %get-tuple-element.266, s32[]{:T(128)S(6)} %select_n.85, s32[64,128]{1,0:T(8,128)S(1)} %copy.60, bf16[64,128]{1,0:T(8,128)(2,1)S(1)} %get-tuple-element.232, bf16[64,128]{1,0:T(8,128)(2,1)S(1)} %get-tuple-element.233, ...), kind=kOutput, calls=%fused_computation.16.clone.1 | convolution fusion | flops 277872640 | bytes 6389764 | tf_op jit(solution)/shard_map/while/body/eval_jaxpr/gco,goh->gch/dot_general | solution.py:45
  158.4 4.3 %fusion.60 = f32[4,128,128]{2,0,1:T(4,128)S(1)} fusion(f32[64,128,128]{2,1,0:T(8,128)S(1)} %fusion.59, f32[4,128,128]{2,0,1:T(4,128)S(1)} %get-tuple-element.251, pred[]{:T(512)S(6)} %compare.3, s32[64]{0:T(128)S(1)} %slice_bitcast_fusion.2), kind=kOutput, calls=%fused_computation.23.clone.1 | convolution fusion | flops 50462976 | bytes 4718849 | tf_op jit(solution)/shard_map/while/body/eval_jaxpr/tg,gch->tch/dot_general | solution.py:47
  162.7 0.1 copy.35
  162.8 0.3 fusion.40
  163.1 0.8 copy.36
  (24 shorter events, 0.2 us)
Async XLA Ops:
  0.0 162.8 %copy-start = (f32[128,128]{1,0:T(8,128)S(1)}, f32[128,128]{1,0:T(8,128)}, u32[]{:S(2)}) copy-start(f32[128,128]{1,0:T(8,128)} %param.21) | copy-start | bytes 196612
  0.0 38.7 %copy-start.1 = (bf16[1,64,128,128]{3,2,1,0:T(8,128)(2,1)S(1)}, bf16[1,64,128,128]{3,2,1,0:T(8,128)(2,1)}, u32[]{:S(2)}) copy-start(bf16[1,64,128,128]{3,2,1,0:T(8,128)(2,1)} %param.12) | copy-start | bytes 6291460
  11.7 18.1 %all-to-all-start = ((bf16[128,3,128]{2,1,0:T(4,128)(2,1)}), bf16[128,3,128]{2,1,0:T(4,128)(2,1)S(1)}, u32[]{:S(2)}, u32[]{:S(2)}) async-start(bf16[128,3,128]{2,1,0:T(4,128)(2,1)} %scatter_fusion), calls=%async_computation | async-start | bytes 262144 | tf_op jit(solution)/shard_map/all_to_all | solution.py:109
  29.8 17.6 %all-to-all-start.1 = ((bf16[128,4,128]{2,1,0:T(4,128)(2,1)}), bf16[128,4,128]{2,1,0:T(4,128)(2,1)S(1)}, u32[]{:S(2)}, u32[]{:S(2)}) async-start(bf16[128,4,128]{2,1,0:T(4,128)(2,1)} %scatter_fusion.1), calls=%async_computation.1 | async-start | bytes 262144 | tf_op jit(solution)/shard_map/all_to_all | solution.py:108
  47.4 99.7 %all-to-all-start.2 = ((bf16[128,128,128]{2,1,0:T(8,128)(2,1)}), bf16[128,128,128]{2,1,0:T(8,128)(2,1)}, u32[]{:S(2)}, u32[]{:S(2)}) async-start(bf16[128,128,128]{2,1,0:T(8,128)(2,1)} %scatter_fusion.2), calls=%async_computation.2 | async-start | bytes 8388608 | tf_op jit(solution)/shard_map/all_to_all | solution.py:107
  147.1 15.7 %copy-start.2 = (f32[4,128]{1,0:T(4,128)S(1)}, f32[4,128]{1,0:T(4,128)}, u32[]{:S(2)}) copy-start(f32[4,128]{1,0:T(4,128)} %param.20) | copy-start | bytes 6148
where the time goes:
time: 165 us; the launch traced here: 164 us
  waiting for transfers between devices  93.7 us (57%)
  local copies, waits for them, and re-layouts  30.1 us (18%)
  starting transfers between devices  19.2 us (12%)
  matrix products  14.9 us (9%)
  other arithmetic  5.23 us (3%)
    all_to_all x1, waiting for transfers between devices, on_device(): lax.all_to_all(send_values, 'space', split_axis=0, concat_axis=0, tiled=T...  93.7 us
    scatter x1, local copies, waits for them, and re-layouts, on_device(): jnp.zeros((slot_total, obs_count, width), jnp.bfloat16).at[slot]  8.72 us
    dot_general x2, matrix products, accumulate(): jnp.einsum('tg,gch->tch', pick, contrib, precision=lax.Precision.HIGHEST)  8.51 us
    scatter x1, local copies, waits for them, and re-layouts, on_device(): send_places = jnp.zeros((slot_total, 3, obs_count), jnp.bfloat16).at[slot...  7.74 us
    scatter x1, local copies, waits for them, and re-layouts, on_device(): jnp.zeros((slot_total, 4, obs_count), jnp.bfloat16).at[slot]  7.39 us
    all_to_all x1, starting transfers between devices, on_device(): lax.all_to_all(send_places, 'space', split_axis=0, concat_axis=0, tiled=T...  7.33 us
    dot_general x2, matrix products, accumulate(): jnp.einsum('gco,goh->gch', table, values, preferred_element_type=jnp.floa...  6.08 us
    all_to_all x1, starting transfers between devices, on_device(): lax.all_to_all(send_values, 'space', split_axis=0, concat_axis=0, tiled=T...  5.99 us
  transfers between devices with their start and end apart: 3, of which 1 were waited for; matrix products, arithmetic and copies ran while one was open for 13% of the time, Pallas kernels for 0%

commit v1 on v0

v1 whole, which is shorter than its diff:
```python
import functools

import jax
import jax.numpy as jnp
from jax import lax
from jax.experimental import pallas as pl
from jax.experimental.pallas import tpu as pltpu
from jax.sharding import PartitionSpec as P

TW = 16
GROUP = 4
STREAMS = 6
ROTATED = 3


MESH = pl.DeviceIdType.MESH


def partial_kernel(
    cells, owner_ref, tile_ref, count_ref, innov_ref, row_ref, col_ref, off_ref, mask_ref,
    send_ref, keep_ref, acc, packed, base_s, weight_s, sem,
):
    blocks, obs, width = innov_ref.shape
    half, rows, _ = packed.shape
    me = lax.axis_index("space")

    def clear(i, carry):
        acc[pl.ds(pl.multiple_of(i * rows, rows), rows), :] = jnp.zeros((rows, width), jnp.float32)
        return carry

    lax.fori_loop(0, 2 * half, clear, 0)
    alive = lax.broadcasted_iota(jnp.int32, (blocks, obs), 0) < count_ref[0]
    live = jnp.where(alive, mask_ref[...].astype(jnp.float32), 0.0)
    row_frac = off_ref[:, 0, :]
    col_frac = off_ref[:, 1, :]
    base_s[...] = row_ref[...] * TW + col_ref[...]
    corners = (
        (1.0 - row_frac) * (1.0 - col_frac),
        (1.0 - row_frac) * col_frac,
        row_frac * (1.0 - col_frac),
        row_frac * col_frac,
    )
    for k, corner in enumerate(corners):
        weight_s[k, :, :] = (corner * live).astype(jnp.bfloat16).astype(jnp.float32)
    cell = lax.broadcasted_iota(jnp.int32, (cells, obs), 0)

    def accumulate(turn, carry):
        sums = []
        for g in range(GROUP):
            b = turn * GROUP + g
            away = cell - base_s[pl.ds(b, 1), :]
            table = jnp.zeros((cells, obs), jnp.float32)
            for k, step in enumerate((0, 1, TW, TW + 1)):
                table = jnp.where(away == step, weight_s[k, pl.ds(b, 1), :], table)
            sums.append(
                jnp.dot(table.astype(jnp.bfloat16), innov_ref[b], preferred_element_type=jnp.float32)
            )
        for g in range(GROUP):
            b = turn * GROUP + g
            slot = lax.bitwise_xor(owner_ref[b], me)
            place = (slot % 2) * half + slot // 2
            at = pl.ds(pl.multiple_of(place * rows + tile_ref[b] * cells, cells), cells)
            acc[at, :] += sums[g]
        return carry

    lax.fori_loop(0, blocks // GROUP, accumulate, 0)

    keep = pltpu.make_async_copy(acc.at[pl.ds(0, half * rows), :], keep_ref, sem.at[0])
    keep.start()

    def pack(i, carry):
        packed[i] = acc[pl.ds(pl.multiple_of((half + i) * rows, rows), rows), :].astype(jnp.bfloat16)
        return carry

    lax.fori_loop(0, half, pack, 0)
    out = pltpu.make_async_copy(packed, send_ref, sem.at[1])
    out.start()
    out.wait()
    keep.wait()


def spread(index, places):
    total = 0
    for j, place in enumerate(places):
        total = total + ((index // (1 << j)) % 2) * (1 << place)
    return total


def plans(bits, rows):
    unit = 16
    count = min(STREAMS, rows // unit)
    edges = [rows // unit * i // count * unit for i in range(count + 1)]
    head = list(range(1, min(1 + ROTATED, bits)))
    tail = list(range(1 + len(head), bits))
    made = []
    for i in range(count):
        turn = i % max(1, len(head))
        made.append((edges[i], edges[i + 1], [0] + head[turn:] + head[:turn] + tail))
    return made


def scatter_kernel(bits, streams, send_ref, keep_ref, out_ref, keep, *scratch):
    count = len(streams)
    recv = [scratch[i * bits : (i + 1) * bits] for i in range(count)]
    sent = [scratch[(count + i) * bits : (count + i + 1) * bits] for i in range(count)]
    send_sem, recv_sem, keep_sem = scratch[2 * count * bits :]
    me = lax.axis_index("space")
    rows = out_ref.shape[0]

    def partner(bit):
        return me + (1 << bit) - 2 * (1 << bit) * ((me // (1 << bit)) % 2)

    barrier = pltpu.get_barrier_semaphore()
    for bit in range(bits):
        pl.semaphore_signal(barrier, inc=1, device_id={"space": partner(bit)}, device_id_type=MESH)
    load = pltpu.make_async_copy(keep_ref, keep, keep_sem)
    load.start()
    pl.semaphore_wait(barrier, bits)

    def copy(i, stage):
        low, high, order = streams[i]
        source = send_ref.at[:, pl.ds(low, high - low), :] if stage == 0 else sent[i][stage]
        return pltpu.make_async_remote_copy(
            src_ref=source,
            dst_ref=recv[i][stage],
            send_sem=send_sem.at[i * bits + stage],
            recv_sem=recv_sem.at[i * bits + stage],
            device_id={"space": partner(order[stage])},
            device_id_type=MESH,
        )

    copies = {}
    for i in range(count):
        copies[i, 0] = copy(i, 0)
        copies[i, 0].start()
    load.wait()
    for stage in range(bits):
        for i, (low, high, order) in enumerate(streams):
            copies[i, stage].wait_recv()
            got = recv[i][stage]
            left = sorted(order[stage + 1 :])
            if not left:
                out_ref[pl.ds(low, high - low), :] = (
                    keep[pl.ds(low, high - low), :] + got[0].astype(jnp.float32)
                )
                continue
            bit = order[stage + 1]
            rest = [b for b in left if b != bit]
            seat = left.index(bit)
            seats = [j for j in range(len(left)) if j != seat]

            def away(r, carry):
                slot = spread(r, [b - 1 for b in rest]) + (1 << (bit - 1))
                at = pl.ds(pl.multiple_of(slot * rows + low, 16), high - low)
                total = keep[at, :] + got[spread(r, seats) + (1 << seat)].astype(jnp.float32)
                sent[i][stage + 1][r] = total.astype(jnp.bfloat16)
                return carry

            def stay(r, carry):
                slot = spread(r, [b - 1 for b in rest])
                at = pl.ds(pl.multiple_of(slot * rows + low, 16), high - low)
                keep[at, :] += got[spread(r, seats)].astype(jnp.float32)
                return carry

            lax.fori_loop(0, 1 << len(rest), away, 0)
            copies[i, stage + 1] = copy(i, stage + 1)
            copies[i, stage + 1].start()
            lax.fori_loop(0, 1 << len(rest), stay, 0)
    for made in copies.values():
        made.wait_send()


def local_sums(
    innovations, block_owner, block_tile, block_count, obs_row, obs_col, offsets, obs_mask, tile_local, cells, peers
):
    blocks, obs, width = innovations.shape
    half, rows = peers // 2, tile_local * cells
    smem = pl.BlockSpec(memory_space=pltpu.SMEM)
    vmem = pl.BlockSpec(memory_space=pltpu.VMEM)
    hbm = pl.BlockSpec(memory_space=pl.ANY)
    return pl.pallas_call(
        functools.partial(partial_kernel, cells),
        out_shape=(
            jax.ShapeDtypeStruct((half, rows, width), jnp.bfloat16),
            jax.ShapeDtypeStruct((half * rows, width), jnp.float32),
        ),
        in_specs=[smem] * 3 + [vmem] * 5,
        out_specs=(hbm, hbm),
        scratch_shapes=[
            pltpu.VMEM((2 * half * rows, width), jnp.float32),
            pltpu.VMEM((half, rows, width), jnp.bfloat16),
            pltpu.VMEM((blocks, obs), jnp.int32),
            pltpu.VMEM((4, blocks, obs), jnp.float32),
            pltpu.SemaphoreType.DMA((2,)),
        ],
        compiler_params=pltpu.CompilerParams(vmem_limit_bytes=56 << 20),
    )(block_owner, block_tile, block_count, innovations, obs_row, obs_col, offsets, obs_mask)


def scatter_sums(send, keep, rows, width, peers):
    bits = peers.bit_length() - 1
    streams = plans(bits, rows)
    hbm = pl.BlockSpec(memory_space=pl.ANY)
    held = [
        pltpu.VMEM((1 << (bits - 1 - stage), high - low, width), jnp.bfloat16)
        for low, high, _ in streams
        for stage in range(bits)
    ]
    outgoing = [
        pltpu.VMEM((1 << (bits - 1 - stage) if stage else 1, high - low, width), jnp.bfloat16)
        for low, high, _ in streams
        for stage in range(bits)
    ]
    return pl.pallas_call(
        functools.partial(scatter_kernel, bits, streams),
        out_shape=jax.ShapeDtypeStruct((rows, width), jnp.float32),
        in_specs=[hbm, hbm],
        out_specs=pl.BlockSpec(memory_space=pltpu.VMEM),
        scratch_shapes=[pltpu.VMEM((peers // 2 * rows, width), jnp.float32)]
        + held
        + outgoing
        + [
            pltpu.SemaphoreType.DMA((len(streams) * bits,)),
            pltpu.SemaphoreType.DMA((len(streams) * bits,)),
            pltpu.SemaphoreType.DMA,
        ],
        compiler_params=pltpu.CompilerParams(
            collective_id=0, has_side_effects=True, vmem_limit_bytes=60 << 20
        ),
    )(send, keep)


def on_device(
    innovations, block_owner, block_tile, block_count, obs_row, obs_col, offsets, obs_mask, sigma, coupling
):
    peers = lax.axis_size("space")
    ens_count = lax.axis_size("ens")
    members = ens_count * innovations.shape[0]
    tile_local, width = sigma.shape
    cells = coupling.shape[0]
    values = innovations[0]
    send, keep = local_sums(
        values, block_owner[:, 0], block_tile, block_count, obs_row, obs_col, offsets, obs_mask,
        tile_local, cells, peers,
    )
    totals = scatter_sums(send, keep, tile_local * cells, width, peers)
    totals = totals.reshape(tile_local, cells, width)
    share = cells // ens_count
    if ens_count > 1:
        totals = lax.psum(totals.astype(jnp.bfloat16), "ens").astype(jnp.float32)
    first = lax.axis_index("ens") * share
    coupling_rows = lax.dynamic_slice_in_dim(coupling, first, share, 0)
    own = lax.dynamic_slice_in_dim(totals, first, share, 1)
    coupled = jnp.einsum("ck,tkh->cth", coupling_rows, totals, precision=lax.Precision.HIGHEST)
    return sigma[None, :, :] * (jnp.transpose(own, (1, 0, 2)) + coupled) / members


def solution(mesh):
    in_specs = (
        P("ens", "space", None, None),
        P("space", None),
        P("space"),
        P("space"),
        P("space", None),
        P("space", None),
        P("space", None, None),
        P("space", None),
        P("space", None),
        P(),
    )
    out_specs = P("ens", "space", None)
    return jax.shard_map(
        on_device, mesh=mesh, in_specs=in_specs, out_specs=out_specs, check_vma=False
    )
```

time: 165 us -> 45.2 us (0.27)
  waiting for transfers between devices: 93.7 us -> 0 us
  Pallas kernels: 0 us -> 40.7 us
  local copies, waits for them, and re-layouts: 30.1 us -> 1.93 us
  starting transfers between devices: 19.2 us -> 0 us
  matrix products: 14.9 us -> 1.54 us
  other arithmetic: 5.23 us -> 0 us
    all_to_all x3 -> x0, waiting for transfers between devices: 93.7 us -> none  [the longest x1 93.7 us: on_device(): lax.all_to_all(send_values, 'space', split_axis=0, concat_axis=0, tiled=T...]
    pallas_call x0 -> x2, Pallas kernels: none -> 40.7 us  [the longest x1 32.2 us: scatter_sums(): pl.pallas_call(functools.partial(scatter_kernel, bits, streams), out_shap...]
    scatter x3 -> x0, local copies, waits for them, and re-layouts: 23.9 us -> none  [the longest x1 8.72 us: on_device(): jnp.zeros((slot_total, obs_count, width), jnp.bfloat16).at[slot]]
    all_to_all x3 -> x0, starting transfers between devices: 19.2 us -> none  [the longest x1 7.33 us: on_device(): lax.all_to_all(send_places, 'space', split_axis=0, concat_axis=0, tiled=T...]
    dot_general x5 -> x1, matrix products: 14.9 us -> 1.54 us  [on_device(): jnp.einsum('ck,tkh->cth', coupling_rows, totals, precision=lax.Precision....]
    broadcast_in_dim x7 -> x0, local copies, waits for them, and re-layouts: 4.43 us -> none  [the longest x1 3.02 us: on_device(): jnp.zeros((slot_total, obs_count, width), jnp.bfloat16).at[slot]]
    mul x2 -> x0, other arithmetic: 1.85 us -> none  [the longest x1 1.01 us: on_device(): (1.0 - row_frac) * (1.0 - col_frac)]
  transfers between devices with their start and end apart: 3 -> 0, of which waited for: 1 -> 0; matrix products, arithmetic and copies ran while one was open for 13% -> 0% of each run, Pallas kernels for 0% -> 0%
where the time goes in v1:
time: 45.2 us; the launch traced here: 44.9 us
  Pallas kernels  40.7 us (90%)
  local copies, waits for them, and re-layouts  1.93 us (4%)
  matrix products  1.54 us (3%)
  between operations  0.74 us (2%)
    pallas_call x1, Pallas kernels, scatter_sums(): pl.pallas_call(functools.partial(scatter_kernel, bits, streams), out_shap...  32.2 us
    pallas_call x1, Pallas kernels, local_sums(): pl.pallas_call(functools.partial(partial_kernel, cells), out_shape=(jax.S...  8.54 us
    dot_general x1, matrix products, on_device(): jnp.einsum('ck,tkh->cth', coupling_rows, totals, precision=lax.Precision....  1.54 us
    reshape x1, local copies, waits for them, and re-layouts, on_device(): totals = totals.reshape(tile_local, cells, width)  1.08 us

profile of v1, /device:TPU:0, one launch (start us, length us, event | category | flops | bytes accessed | tf_op | source)
XLA Modules:
  0.0 44.9 jit_solution(4078392416776599663)
XLA Ops:
  0.0 0.0 copy-start
  0.7 8.5 %shard_map.100 = (bf16[16,512,128]{2,1,0:T(8,128)(2,1)}, f32[8192,128]{1,0:T(8,128)}) custom-call(s32[64]{0:T(128)} %bitcast.18, s32[64]{0:T(128)} %tile_ref.1, s32[1]{0:T(128)S(6)} %copy.15.count_ref, bf16[64,128,128]{2,1,0:T(8,128)(2,1)} %bitcast.17, s32[64,128]{1,0:T(8,128)} %row_ref.1, s32[64,128]{1,0:T(8,128)} %col_ref.1, f32[64,2,128]{2,1,0:T(2,128)} %off_ref.1, ...), custom_call_target="tpu_custom_call" | custom-call | tf_op jit(solution)/shard_map/pallas_call | solution.py:181
  9.2 0.0 copy-start.1
  9.2 32.2 %shard_map.101 = f32[512,128]{1,0:T(8,128)} custom-call(bf16[16,512,128]{2,1,0:T(8,128)(2,1)} %get-tuple-element.7.send_ref, f32[8192,128]{1,0:T(8,128)} %get-tuple-element.8.keep_ref), custom_call_target="tpu_custom_call" | custom-call | tf_op jit(solution)/shard_map/pallas_call | solution.py:214
  41.4 1.1 %copy.11 = f32[4,128,128]{1,2,0:T(8,128)S(1)} copy(f32[4,128,128]{2,1,0:T(8,128)} %bitcast.15) | data formatting | bytes 524288 | tf_op jit(solution)/shard_map/reshape | solution.py:247
  42.5 0.0 copy-done
  42.5 0.0 copy-done.1
  42.5 1.5 %fusion.1 = f32[128,4,128]{0,2,1:T(8,128)S(1)} fusion(f32[4,128,128]{2,1,0:T(8,128)} %bitcast.16, f32[4,128,128]{1,2,0:T(8,128)S(1)} %copy.11, f32[4,128]{1,0:T(4,128)S(1)} %copy-done.1, f32[128,128]{1,0:T(8,128)S(1)} %copy-done), kind=kOutput, calls=%fused_computation.2 | convolution fusion | flops 100794368 | bytes 854016 | tf_op jit(solution)/shard_map/ck,tkh->cth/dot_general | solution.py:254
  44.1 0.8 %copy.13 = f32[128,4,128]{2,1,0:T(4,128)} copy(f32[128,4,128]{0,2,1:T(8,128)S(1)} %fusion.1) | data formatting | bytes 524288 | tf_op jit(solution)/shard_map/mul | solution.py:255
Async XLA Ops:
  0.0 42.5 %copy-start = (f32[128,128]{1,0:T(8,128)S(1)}, f32[128,128]{1,0:T(8,128)}, u32[]{:S(2)}) copy-start(f32[128,128]{1,0:T(8,128)} %param.19) | copy-start | bytes 196612
  9.2 33.3 %copy-start.1 = (f32[4,128]{1,0:T(4,128)S(1)}, f32[4,128]{1,0:T(4,128)}, u32[]{:S(2)}) copy-start(f32[4,128]{1,0:T(4,128)} %param.18) | copy-start | bytes 6148

commit v2 on v1

v2 whole, which is shorter than its diff:
```python
import functools

import jax
import jax.numpy as jnp
from jax import lax
from jax.experimental import pallas as pl
from jax.experimental.pallas import tpu as pltpu
from jax.sharding import PartitionSpec as P

TW = 16
GROUP = 4
STREAMS = 6
ROTATED = 3


MESH = pl.DeviceIdType.MESH


def partial_kernel(
    cells, owner_ref, tile_ref, count_hbm, innov_hbm, row_ref, col_ref, off_ref, mask_ref,
    send_ref, keep_ref, acc, innov_ref, count_ref, base_s, weight_s, sem, count_sem,
):
    blocks, obs, width = innov_ref.shape
    half, rows, _ = send_ref.shape
    me = lax.axis_index("space")
    load = pltpu.make_async_copy(innov_hbm, innov_ref, sem)
    load.start()
    number = pltpu.make_async_copy(count_hbm, count_ref, count_sem)
    number.start()

    def clear(i, carry):
        acc[pl.ds(pl.multiple_of(i * rows, rows), rows), :] = jnp.zeros((rows, width), jnp.float32)
        return carry

    lax.fori_loop(0, 2 * half, clear, 0)
    number.wait()
    alive = lax.broadcasted_iota(jnp.int32, (blocks, obs), 0) < count_ref[0]
    live = jnp.where(alive, mask_ref[...].astype(jnp.float32), 0.0)
    row_frac = off_ref[:, 0, :]
    col_frac = off_ref[:, 1, :]
    base_s[...] = row_ref[...] * TW + col_ref[...]
    corners = (
        (1.0 - row_frac) * (1.0 - col_frac),
        (1.0 - row_frac) * col_frac,
        row_frac * (1.0 - col_frac),
        row_frac * col_frac,
    )
    for k, corner in enumerate(corners):
        weight_s[k, :, :] = (corner * live).astype(jnp.bfloat16).astype(jnp.float32)
    cell = lax.broadcasted_iota(jnp.int32, (cells, obs), 0)

    def accumulate(turn, carry):
        sums = []
        for g in range(GROUP):
            b = turn * GROUP + g
            away = cell - base_s[pl.ds(b, 1), :]
            table = jnp.zeros((cells, obs), jnp.float32)
            for k, step in enumerate((0, 1, TW, TW + 1)):
                table = jnp.where(away == step, weight_s[k, pl.ds(b, 1), :], table)
            sums.append(
                jnp.dot(table.astype(jnp.bfloat16), innov_ref[b], preferred_element_type=jnp.float32)
            )
        for g in range(GROUP):
            b = turn * GROUP + g
            slot = lax.bitwise_xor(owner_ref[b], me)
            place = (slot % 2) * half + slot // 2
            at = pl.ds(pl.multiple_of(place * rows + tile_ref[b] * cells, cells), cells)
            acc[at, :] += sums[g]
        return carry

    load.wait()
    lax.fori_loop(0, blocks // GROUP, accumulate, 0)

    def pack(i, carry):
        own = pl.ds(pl.multiple_of(i * rows, rows), rows)
        send_ref[i] = acc[pl.ds(pl.multiple_of((half + i) * rows, rows), rows), :].astype(jnp.bfloat16)
        keep_ref[own, :] = acc[own, :].astype(keep_ref.dtype)
        return carry

    lax.fori_loop(0, half, pack, 0)


def spread(index, places):
    total = 0
    for j, place in enumerate(places):
        total = total + ((index // (1 << j)) % 2) * (1 << place)
    return total


def plans(bits, rows):
    unit = 16
    count = min(STREAMS, rows // unit)
    edges = [rows // unit * i // count * unit for i in range(count + 1)]
    head = list(range(1, min(1 + ROTATED, bits)))
    tail = list(range(1 + len(head), bits))
    made = []
    for i in range(count):
        turn = i % max(1, len(head))
        made.append((edges[i], edges[i + 1], [0] + head[turn:] + head[:turn] + tail))
    return made


def scatter_kernel(bits, streams, tail, send_ref, keep_ref, *rest):
    if tail:
        sigma_ref, coupling_ref, *rest = rest
    out_ref, *rest = rest
    count = len(streams)
    recv, rest = [rest[i * bits : (i + 1) * bits] for i in range(count)], rest[count * bits :]
    sent, rest = [rest[i * (bits - 1) : (i + 1) * (bits - 1)] for i in range(count)], rest[count * (bits - 1) :]
    kept, (total_ref, send_sem, recv_sem) = rest[:count], rest[count:]
    me = lax.axis_index("space")
    rows, width = total_ref.shape

    def partner(bit):
        return me + (1 << bit) - 2 * (1 << bit) * ((me // (1 << bit)) % 2)

    barrier = pltpu.get_barrier_semaphore()
    for bit in range(bits):
        pl.semaphore_signal(barrier, inc=1, device_id={"space": partner(bit)}, device_id_type=MESH)
    pl.semaphore_wait(barrier, bits)

    def copy(i, stage):
        low, high, order = streams[i]
        source = send_ref.at[:, pl.ds(low, high - low), :] if stage == 0 else sent[i][stage - 1]
        return pltpu.make_async_remote_copy(
            src_ref=source,
            dst_ref=recv[i][stage],
            send_sem=send_sem.at[i * bits + stage],
            recv_sem=recv_sem.at[i * bits + stage],
            device_id={"space": partner(order[stage])},
            device_id_type=MESH,
        )

    copies = {}
    for i in range(count):
        copies[i, 0] = copy(i, 0)
        copies[i, 0].start()
    for stage in range(bits):
        for i, (low, high, order) in enumerate(streams):
            copies[i, stage].wait_recv()
            got = recv[i][stage]
            left = sorted(order[stage + 1 :])
            held = sorted(order[2:])
            if not left:
                total_ref[pl.ds(low, high - low), :] = kept[i][0] + got[0].astype(jnp.float32)
                continue
            bit = order[stage + 1]
            others = [b for b in left if b != bit]
            seats = [left.index(b) for b in others]
            seat = left.index(bit)

            def have(r, upper):
                if stage == 0:
                    slot = spread(r, [b - 1 for b in others]) + upper * (1 << (bit - 1))
                    return keep_ref[pl.ds(pl.multiple_of(slot * rows + low, 16), high - low), :].astype(jnp.float32)
                return kept[i][spread(r, [held.index(b) for b in others]) + upper * (1 << held.index(bit))]

            def away(r, carry):
                total = have(r, 1) + got[spread(r, seats) + (1 << seat)].astype(jnp.float32)
                sent[i][stage][r] = total.astype(jnp.bfloat16)
                return carry

            def stay(r, carry):
                kept[i][spread(r, [held.index(b) for b in others])] = have(r, 0) + got[spread(r, seats)].astype(
                    jnp.float32
                )
                return carry

            lax.fori_loop(0, 1 << len(others), away, 0)
            copies[i, stage + 1] = copy(i, stage + 1)
            copies[i, stage + 1].start()
            lax.fori_loop(0, 1 << len(others), stay, 0)
    if tail:
        cells, tiles, _ = out_ref.shape
        mean = [total_ref[pl.ds(t * cells, cells), :] for t in range(tiles)]
        coupled = jnp.dot(
            coupling_ref[...], jnp.concatenate(mean, axis=1),
            precision=lax.Precision.HIGHEST, preferred_element_type=jnp.float32,
        )
        for t in range(tiles):
            out_ref[:, t, :] = sigma_ref[pl.ds(t, 1), :] * (mean[t] + coupled[:, t * width : (t + 1) * width])
    else:
        out_ref[...] = total_ref[...]
    for made in copies.values():
        made.wait_send()


def local_sums(
    innovations, block_owner, block_tile, block_count, obs_row, obs_col, offsets, obs_mask, tile_local, cells, peers
):
    blocks, obs, width = innovations.shape
    half, rows = peers // 2, tile_local * cells
    kind = jnp.float32 if peers * rows * width <= 1 << 22 else jnp.bfloat16
    smem = pl.BlockSpec(memory_space=pltpu.SMEM)
    vmem = pl.BlockSpec(memory_space=pltpu.VMEM)
    hbm = pl.BlockSpec(memory_space=pltpu.HBM)
    return pl.pallas_call(
        functools.partial(partial_kernel, cells),
        out_shape=(
            pltpu.VMEM((half, rows, width), jnp.bfloat16),
            pltpu.VMEM((half * rows, width), kind),
        ),
        in_specs=[smem] * 2 + [hbm, hbm] + [vmem] * 4,
        out_specs=(vmem, vmem),
        scratch_shapes=[
            pltpu.VMEM((2 * half * rows, width), jnp.float32),
            pltpu.VMEM((blocks, obs, width), jnp.bfloat16),
            pltpu.SMEM((1,), jnp.int32),
            pltpu.VMEM((blocks, obs), jnp.int32),
            pltpu.VMEM((4, blocks, obs), jnp.float32),
            pltpu.SemaphoreType.DMA,
            pltpu.SemaphoreType.DMA,
        ],
        compiler_params=pltpu.CompilerParams(vmem_limit_bytes=limit(peers, rows, width, -3, 62)),
    )(block_owner, block_tile, block_count, innovations, obs_row, obs_col, offsets, obs_mask)


def limit(peers, rows, width, whole, more):
    return peers * rows * width * whole + (more << 20)


def scatter_sums(send, keep, sigma, coupling, tile_local, cells, peers, tail):
    bits = peers.bit_length() - 1
    width, rows = sigma.shape[1], tile_local * cells
    streams = plans(bits, rows)
    vmem = pl.BlockSpec(memory_space=pltpu.VMEM)

    def room(first, kind):
        return [
            pltpu.VMEM((1 << (bits - 1 - stage), high - low, width), kind)
            for low, high, _ in streams
            for stage in range(first, bits)
        ]

    kept = [pltpu.VMEM((1 << (bits - 2), high - low, width), jnp.float32) for low, high, _ in streams]
    shape = (cells, tile_local, width) if tail else (rows, width)
    return pl.pallas_call(
        functools.partial(scatter_kernel, bits, streams, tail),
        out_shape=jax.ShapeDtypeStruct(shape, jnp.float32),
        in_specs=[vmem] * (4 if tail else 2),
        out_specs=vmem,
        scratch_shapes=room(0, jnp.bfloat16)
        + room(1, jnp.bfloat16)
        + kept
        + [
            pltpu.VMEM((rows, width), jnp.float32),
            pltpu.SemaphoreType.DMA((len(streams) * bits,)),
            pltpu.SemaphoreType.DMA((len(streams) * bits,)),
        ],
        compiler_params=pltpu.CompilerParams(
            collective_id=0, has_side_effects=True, vmem_limit_bytes=limit(peers, rows, width, 4, 4)
        ),
    )(send, keep, *((sigma, coupling) if tail else ()))


def on_device(
    innovations, block_owner, block_tile, block_count, obs_row, obs_col, offsets, obs_mask, sigma, coupling
):
    peers = lax.axis_size("space")
    ens_count = lax.axis_size("ens")
    members = ens_count * innovations.shape[0]
    tile_local, width = sigma.shape
    cells = coupling.shape[0]
    values = innovations[0]
    send, keep = local_sums(
        values, block_owner[:, 0], block_tile, block_count, obs_row, obs_col, offsets, obs_mask,
        tile_local, cells, peers,
    )
    totals = scatter_sums(send, keep, sigma, coupling, tile_local, cells, peers, members == 1)
    if members == 1:
        return totals
    totals = totals.reshape(tile_local, cells, width)
    share = cells // ens_count
    if ens_count > 1:
        totals = lax.psum(totals.astype(jnp.bfloat16), "ens").astype(jnp.float32)
    first = lax.axis_index("ens") * share
    coupling_rows = lax.dynamic_slice_in_dim(coupling, first, share, 0)
    own = lax.dynamic_slice_in_dim(totals, first, share, 1)
    coupled = jnp.einsum("ck,tkh->cth", coupling_rows, totals, precision=lax.Precision.HIGHEST)
    return sigma[None, :, :] * (jnp.transpose(own, (1, 0, 2)) + coupled) / members


def solution(mesh):
    in_specs = (
        P("ens", "space", None, None),
        P("space", None),
        P("space"),
        P("space"),
        P("space", None),
        P("space", None),
        P("space", None, None),
        P("space", None),
        P("space", None),
        P(),
    )
    out_specs = P("ens", "space", None)
    return jax.shard_map(
        on_device, mesh=mesh, in_specs=in_specs, out_specs=out_specs, check_vma=False
    )
```

time: 45.2 us -> 39.9 us (0.88)
  Pallas kernels: 40.7 us -> 38.2 us
  matrix products: 1.54 us -> 0 us
  local copies, waits for them, and re-layouts: 1.93 us -> 0.71 us
    pallas_call x2, Pallas kernels: 40.7 us -> 38.2 us  [the longest x1 31.7 us: scatter_sums(): pl.pallas_call(functools.partial(scatter_kernel, bits, streams, tail), ou...]
    dot_general x1 -> x0, matrix products: 1.54 us -> none  [on_device(): jnp.einsum('ck,tkh->cth', coupling_rows, totals, precision=lax.Precision....]
    reshape x1 -> x0, local copies, waits for them, and re-layouts: 1.08 us -> none  [on_device(): totals = totals.reshape(tile_local, cells, width)]
    mul x1 -> x0, local copies, waits for them, and re-layouts: 0.84 us -> none  [on_device(): sigma[None, :, :] * (jnp.transpose(own, (1, 0, 2)) + coupled) / members]
    unnamed x4 -> x5, local copies, waits for them, and re-layouts: 0.01 us -> 0.71 us
where the time goes in v2:
time: 39.9 us; the launch traced here: 39.7 us
  Pallas kernels  38.2 us (96%)
  between operations  0.72 us (2%)
  local copies, waits for them, and re-layouts  0.71 us (2%)
    pallas_call x1, Pallas kernels, scatter_sums(): pl.pallas_call(functools.partial(scatter_kernel, bits, streams, tail), ou...  31.7 us
    pallas_call x1, Pallas kernels, local_sums(): pl.pallas_call(functools.partial(partial_kernel, cells), out_shape=(pltpu...  6.48 us

profile of v2, /device:TPU:0, one launch (start us, length us, event | category | flops | bytes accessed | tf_op | source)
XLA Modules:
  0.0 39.7 jit_solution(3174557112539995079)
XLA Ops:
  0.0 0.0 copy-start
  0.0 0.0 copy-start.1
  0.7 6.5 %shard_map.100 = (bf16[16,512,128]{2,1,0:T(8,128)(2,1)S(1)}, f32[8192,128]{1,0:T(8,128)S(1)}) custom-call(s32[64]{0:T(128)} %bitcast.3, s32[64]{0:T(128)} %tile_ref.1, s32[1]{0:T(128)S(6)} %copy.12.count_hbm, bf16[64,128,128]{2,1,0:T(8,128)(2,1)} %bitcast.2, s32[64,128]{1,0:T(8,128)} %row_ref.1, s32[64,128]{1,0:T(8,128)} %col_ref.1, f32[64,2,128]{2,1,0:T(2,128)} %off_ref.1, ...), custom_call_target="tpu_custom_call" | custom-call | tf_op jit(solution)/shard_map/pallas_call | solution.py:197
  7.2 0.0 copy-done
  7.2 0.0 copy-done.1
  7.2 31.7 %shard_map.101 = f32[128,4,128]{2,1,0:T(4,128)S(1)} custom-call(bf16[16,512,128]{2,1,0:T(8,128)(2,1)S(1)} %get-tuple-element.7.send_ref, f32[8192,128]{1,0:T(8,128)S(1)} %get-tuple-element.8.keep_ref, f32[4,128]{1,0:T(4,128)S(1)} %copy-done.1, f32[128,128]{1,0:T(8,128)S(1)} %copy-done), custom_call_target="tpu_custom_call" | custom-call | tf_op jit(solution)/shard_map/pallas_call | solution.py:237
  38.9 0.7 %copy.13 = f32[128,4,128]{2,1,0:T(4,128)} copy(f32[128,4,128]{2,1,0:T(4,128)S(1)} %shard_map.101) | data formatting | bytes 524288
Async XLA Ops:
  0.0 7.2 %copy-start = (f32[128,128]{1,0:T(8,128)S(1)}, f32[128,128]{1,0:T(8,128)}, u32[]{:S(2)}) copy-start(f32[128,128]{1,0:T(8,128)} %rest_1_.1) | copy-start | bytes 196612
  0.0 7.2 %copy-start.1 = (f32[4,128]{1,0:T(4,128)S(1)}, f32[4,128]{1,0:T(4,128)}, u32[]{:S(2)}) copy-start(f32[4,128]{1,0:T(4,128)} %rest_0_.1) | copy-start | bytes 6148

commit v3 on v2

--- a/solution.py
+++ b/solution.py
@@ -8,9 +8,9 @@
 from jax.sharding import PartitionSpec as P
 
 TW = 16
-GROUP = 4
-STREAMS = 6
-ROTATED = 3
+GROUP = 16
+PIECES = (1, 1, 1)
+SHARES = (1, 1, 1)
 
 
 MESH = pl.DeviceIdType.MESH
@@ -89,14 +89,17 @@
 
 def plans(bits, rows):
     unit = 16
-    count = min(STREAMS, rows // unit)
-    edges = [rows // unit * i // count * unit for i in range(count + 1)]
-    head = list(range(1, min(1 + ROTATED, bits)))
+    head = list(range(1, min(1 + len(SHARES), bits)))
     tail = list(range(1 + len(head), bits))
-    made = []
-    for i in range(count):
-        turn = i % max(1, len(head))
-        made.append((edges[i], edges[i + 1], [0] + head[turn:] + head[:turn] + tail))
+    sizes = [(piece * SHARES[turn], turn) for piece in PIECES for turn in range(len(head))]
+    whole = sum(size for size, _ in sizes)
+    made, done, low = [], 0, 0
+    for size, turn in sizes:
+        done += size
+        high = (2 * done * (rows // unit) + whole) // (2 * whole) * unit
+        if high > low:
+            made.append((low, high, [0] + head[turn:] + head[:turn] + tail))
+        low = high
     return made
 
 

time: 39.9 us -> 36.8 us (0.922)
  Pallas kernels: 38.2 us -> 35.1 us
    pallas_call x1, Pallas kernels: 31.7 us -> 30.1 us  [scatter_sums(): pl.pallas_call(functools.partial(scatter_kernel, bits, streams, tail), ou...]
    pallas_call x1, Pallas kernels: 6.48 us -> 4.99 us  [local_sums(): pl.pallas_call(functools.partial(partial_kernel, cells), out_shape=(pltpu...]
where the time goes in v3:
time: 36.8 us; the launch traced here: 36.6 us
  Pallas kernels  35.1 us (95%)
  between operations  0.72 us (2%)
  local copies, waits for them, and re-layouts  0.71 us (2%)
    pallas_call x1, Pallas kernels, scatter_sums(): pl.pallas_call(functools.partial(scatter_kernel, bits, streams, tail), ou...  30.1 us
    pallas_call x1, Pallas kernels, local_sums(): pl.pallas_call(functools.partial(partial_kernel, cells), out_shape=(pltpu...  4.99 us

profile of v3, /device:TPU:0, one launch (start us, length us, event | category | flops | bytes accessed | tf_op | source)
XLA Modules:
  0.0 36.6 jit_solution(14575391182814735835)
XLA Ops:
  0.0 0.0 copy-start
  0.0 0.0 copy-start.1
  0.7 5.0 %shard_map.100 = (bf16[16,512,128]{2,1,0:T(8,128)(2,1)S(1)}, f32[8192,128]{1,0:T(8,128)S(1)}) custom-call(s32[64]{0:T(128)} %bitcast.3, s32[64]{0:T(128)} %tile_ref.1, s32[1]{0:T(128)S(6)} %copy.12.count_hbm, bf16[64,128,128]{2,1,0:T(8,128)(2,1)} %bitcast.2, s32[64,128]{1,0:T(8,128)} %row_ref.1, s32[64,128]{1,0:T(8,128)} %col_ref.1, f32[64,2,128]{2,1,0:T(2,128)} %off_ref.1, ...), custom_call_target="tpu_custom_call" | custom-call | tf_op jit(solution)/shard_map/pallas_call | solution.py:200
  5.7 0.0 copy-done
  5.7 0.0 copy-done.1
  5.7 30.1 %shard_map.101 = f32[128,4,128]{2,1,0:T(4,128)S(1)} custom-call(bf16[16,512,128]{2,1,0:T(8,128)(2,1)S(1)} %get-tuple-element.7.send_ref, f32[8192,128]{1,0:T(8,128)S(1)} %get-tuple-element.8.keep_ref, f32[4,128]{1,0:T(4,128)S(1)} %copy-done.1, f32[128,128]{1,0:T(8,128)S(1)} %copy-done), custom_call_target="tpu_custom_call" | custom-call | tf_op jit(solution)/shard_map/pallas_call | solution.py:240
  35.8 0.7 %copy.13 = f32[128,4,128]{2,1,0:T(4,128)} copy(f32[128,4,128]{2,1,0:T(4,128)S(1)} %shard_map.101) | data formatting | bytes 524288
Async XLA Ops:
  0.0 5.7 %copy-start = (f32[128,128]{1,0:T(8,128)S(1)}, f32[128,128]{1,0:T(8,128)}, u32[]{:S(2)}) copy-start(f32[128,128]{1,0:T(8,128)} %rest_1_.1) | copy-start | bytes 196612
  0.0 5.7 %copy-start.1 = (f32[4,128]{1,0:T(4,128)S(1)}, f32[4,128]{1,0:T(4,128)}, u32[]{:S(2)}) copy-start(f32[4,128]{1,0:T(4,128)} %rest_0_.1) | copy-start | bytes 6148
